TPU v7x, 32 devices: a whole 2x2x4 slice. The times are simulated.
32 devices in a mesh: py: 4 (over y, core), pz: 8 (over z, x).
Axes of the slice: x: 2, y: 2, z: 4, core: 2. Of those that a mesh axis runs over, the one named last changes fastest.
Arguments:
- wavefunctions: float32 [2, 8, 128, 128, 128], P(None, None, 'pz', 'py'), may hold values from -6 to 6
- potential: float32 [128, 128, 128], P('pz', 'py'), may hold values from -4 to 4
- cutoff_sq: int32 [1], replicated, may hold values from 2304 to 4096
- locked_mask: int32 [8], replicated, may hold values 0 or 1
Outputs:
- applied: float32 [2, 8, 128, 128, 128], P(None, None, 'pz', 'py')
- rayleigh: float32 [8], replicated
- residual_norm: float32 [8], replicated
All inputs are finite; a program needn't handle non-finite values.
Results may differ from a plain program's by a relative error of at most 0.00005.
Values sent between devices are 32-bit elements; how exact they have to be, the bound alone decides.
A program may use at most 64 MiB of HBM per device.

v0:
```python
import math
import jax
import jax.numpy as jnp
from jax import lax
from jax.sharding import PartitionSpec as P


def make_tables(length, inverse):
    counter = jnp.arange(length, dtype=jnp.int32)
    phase = counter[:, None] * counter[None, :] % length
    angle = 2.0 * math.pi / length * phase.astype(jnp.float32)
    if inverse:
        return (jnp.cos(angle) / length, jnp.sin(angle) / length)
    return (jnp.cos(angle), -jnp.sin(angle))


def transform_axis(field, axis, tables):
    cosines, sines = tables
    letters = "abcdefgh"[: field.ndim - 1]
    place = axis - 1
    source = letters[:place] + "n" + letters[place + 1 :]
    target = letters[:place] + "k" + letters[place + 1 :]
    form = source + ",kn->" + target
    real_part = field[0]
    imag_part = field[1]
    high = lax.Precision.HIGHEST
    out_real = jnp.einsum(form, real_part, cosines, precision=high) - jnp.einsum(
        form, imag_part, sines, precision=high
    )
    out_imag = jnp.einsum(form, real_part, sines, precision=high) + jnp.einsum(
        form, imag_part, cosines, precision=high
    )
    return jnp.stack([out_real, out_imag])


def signed_square(counter, length):
    signed = jnp.where(counter < length // 2, counter, counter - length)
    return signed * signed


def kinetic_table(first_sq, second_sq, third_sq, cutoff_sq, length):
    total = first_sq[:, None, None] + second_sq[None, :, None] + third_sq[None, None, :]
    keep = (total <= cutoff_sq[0]).astype(jnp.float32)
    return 0.5 * (math.pi / length) ** 2 * total.astype(jnp.float32) * keep


def slab_kinetic(field, cutoff_sq, forward, inverse):
    parts, bands, rows_z, rows_y, length = field.shape
    size_y = lax.axis_size("py")
    size_z = lax.axis_size("pz")
    along_x = transform_axis(field, 4, forward)
    flat = jnp.moveaxis(along_x, 1, 3).reshape(parts, rows_z, rows_y, bands * length)
    planes = lax.all_to_all(
        lax.all_to_all(flat, "py", split_axis=3, concat_axis=2, tiled=True),
        "pz",
        split_axis=3,
        concat_axis=1,
        tiled=True,
    )
    width = planes.shape[3]
    start = lax.axis_index("py") * (bands * length // size_y) + lax.axis_index("pz") * width
    column = start + jnp.arange(width, dtype=jnp.int32)
    full_counter = jnp.arange(length, dtype=jnp.int32)
    full_sq = signed_square(full_counter, length)
    kinetic = kinetic_table(
        full_sq, full_sq, signed_square(column % length, length), cutoff_sq, length
    )
    spectrum = transform_axis(transform_axis(planes, 1, forward), 2, forward) * kinetic
    spatial = transform_axis(transform_axis(spectrum, 2, inverse), 1, inverse)
    returned = lax.all_to_all(
        lax.all_to_all(spatial, "py", split_axis=2, concat_axis=3, tiled=True),
        "pz",
        split_axis=1,
        concat_axis=3,
        tiled=True,
    )
    ordered = returned.reshape(parts, rows_z, rows_y, size_z, size_y, width)
    ordered = jnp.swapaxes(ordered, 3, 4).reshape(parts, rows_z, rows_y, bands, length)
    return transform_axis(jnp.moveaxis(ordered, 3, 1), 4, inverse)


def apply_kinetic(field, cutoff_sq, forward, inverse):
    return slab_kinetic(field, cutoff_sq, forward, inverse)


def body(wavefunctions, potential, cutoff_sq, locked_mask):
    length = wavefunctions.shape[4]
    forward = make_tables(length, False)
    inverse = make_tables(length, True)
    blocks = wavefunctions.shape[1] // 4

    def one_block(block, result):
        piece = lax.dynamic_slice_in_dim(wavefunctions, block * 4, 4, 1)
        done = apply_kinetic(piece, cutoff_sq, forward, inverse)
        return lax.dynamic_update_slice_in_dim(result, done, block * 4, 1)

    kinetic_part = lax.fori_loop(0, blocks, one_block, jnp.zeros_like(wavefunctions))
    applied = kinetic_part + potential[None, None] * wavefunctions
    norm_local = jnp.sum(wavefunctions * wavefunctions, axis=(0, 2, 3, 4))
    correlation_local = jnp.sum(wavefunctions * applied, axis=(0, 2, 3, 4))
    norm_sq, correlation = lax.psum((norm_local, correlation_local), ("py", "pz"))
    rayleigh = correlation / norm_sq
    residual = applied - rayleigh[None, :, None, None, None] * wavefunctions
    residual_sq = lax.psum(jnp.sum(residual * residual, axis=(0, 2, 3, 4)), ("py", "pz"))
    residual_norm = jnp.sqrt(residual_sq / norm_sq) * (1.0 - locked_mask.astype(jnp.float32))
    return (applied, rayleigh, residual_norm)


def solution(mesh):
    in_specs = (P(None, None, "pz", "py", None), P("pz", "py", None), P(), P())
    out_specs = (P(None, None, "pz", "py", None), P(), P())
    return jax.shard_map(body, mesh=mesh, in_specs=in_specs, out_specs=out_specs, check_vma=False)
```

profile of v0, /device:TPU:0, one launch (start us, length us, event | category | flops | bytes accessed | tf_op | source)
XLA Modules:
  0.0 693.6 jit_solution(16688748125790381216)
XLA Ops:
  0.6 2.5 broadcast_in_dim.14
  3.2 599.9 %while.18 = (s32[]{:T(128)}, f32[2,8,16,32,128]{4,3,2,1,0:T(8,128)}, f32[2,8,16,32,128]{4,3,2,1,0:T(8,128)}, s32[1]{0:T(128)}, s32[]{:T(128)}, /*index=5*/s32[]{...) while((s32[]{:T(128)}, ...), condition=%wide.region_1.2_spmd.clone.clone, body=%wide.region_0.1_spmd.clone.clone.sunk | while | flops 9676570624 | bytes 232916592 | solution.py:97
  3.2 2.5 fusion.346
  5.7 2.4 fusion.344
  8.1 2.5 fusion.347
  10.6 2.5 fusion.345
  13.3 7.5 %copy.142 = f32[2,16,32,4,128]{2,1,0,4,3:T(8,128)} copy(f32[2,16,32,4,128]{4,2,1,3,0:T(8,128)S(1)} %maximum_bitcast_fusion.2) | data formatting | bytes 4194304 | tf_op jit(solution)/shard_map/while/body/eval_jaxpr/reshape | solution.py:52
  20.7 6.1 reshape.143
  26.9 30.2 %all_to_all.204 = f32[4,1,131072]{2,1,0:T(1,128)} all-to-all(f32[4,1,131072]{2,1,0:T(1,128)S(1)} %reshape.143), channel_id=1, replica_groups=mesh['py'=4,'pz'=8] {'py'}, dimensions={0} | all-to-all | bytes 4194304 | tf_op jit(solution)/shard_map/while/body/eval_jaxpr/all_to_all | solution.py:54
  57.6 7.7 %reduce.4 = f32[4,131072]{1,0:T(4,128)S(1)} reduce(f32[4,1,131072]{2,1,0:T(1,128)} %all_to_all.204, f32[]{:T(128)} %broadcast.656), dimensions={1}, to_apply=%all_to_all.178.reduce_sub_computation | reduce | bytes 4194308 | tf_op jit(solution)/shard_map/while/body/eval_jaxpr/all_to_all | solution.py:54
  65.3 6.1 reshape.144
  71.4 5.2 copy.143
  78.2 3.1 copy.145
  81.3 6.9 all-to-all-start.1
  89.3 46.3 %all-to-all-done.1 = f32[2,16,128,128]{2,1,0,3:T(8,128)S(1)} async-done(((f32[2,16,128,128]{2,1,0,3:T(8,128)}), f32[2,16,128,128]{2,1,0,3:T(8,128)S(1)}, u32[]{:S(2)}, u32[]{:S(2)}) %all-to-all-start.1) | async-done | bytes 2097184 | tf_op jit(solution)/shard_map/while/body/eval_jaxpr/all_to_all | solution.py:53
  139.7 2.2 fusion.349
  144.7 2.4 fusion.350
  152.2 2.1 fusion.354
  165.6 2.0 fusion.365
  167.5 1.9 fusion.367
  170.9 28.1 %all_to_all.205 = f32[2,128,128,16]{1,3,0,2:T(8,128)S(1)} all-to-all(f32[2,128,128,16]{1,3,0,2:T(8,128)S(1)} %copy.151), channel_id=1, replica_groups=mesh['py'=4,'pz'=8] {'py'}, dimensions={2} | all-to-all | bytes 4194304 | tf_op jit(solution)/shard_map/while/body/eval_jaxpr/all_to_all | solution.py:71
  199.3 4.5 copy.153
  203.8 7.2 %reshape.145 = f32[8,1,65536]{2,1,0:T(1,128)} reshape(f32[128,2,32,64]{3,2,1,0:T(8,128)} %bitcast.327) | data formatting | bytes 4194304 | tf_op jit(solution)/shard_map/while
  211.0 3.9 all-to-all-start.3
  214.9 48.0 %all-to-all-done.3 = f32[8,1,65536]{2,1,0:T(1,128)S(1)} async-done(((f32[8,1,65536]{2,1,0:T(1,128)}), f32[8,1,65536]{2,1,0:T(1,128)S(1)}, u32[]{:S(2)}, u32[]{:S(2)}) %all-to-all-start.3) | async-done | bytes 2097184 | tf_op jit(solution)/shard_map/while/body/eval_jaxpr/all_to_all | solution.py:70
  264.8 7.2 %reduce.5 = f32[8,65536]{1,0:T(8,128)S(1)} reduce(f32[8,1,65536]{2,1,0:T(1,128)} %copy-done, f32[]{:T(128)} %broadcast.657), dimensions={1}, to_apply=%all_to_all.189.reduce_sub_computation | reduce | bytes 4194308 | tf_op jit(solution)/shard_map/while/body/eval_jaxpr/all_to_all | solution.py:70
  272.0 3.6 reshape.146
  275.6 7.0 %copy.154 = f32[2,16,32,8,64]{2,4,3,1,0:T(8,128)} copy(f32[2,16,32,8,64]{4,2,0,1,3:T(8,128)} %bitcast.326) | data formatting | bytes 4194304 | tf_op jit(solution)/shard_map/while/body/eval_jaxpr/all_to_all | solution.py:70
  282.6 7.9 %copy.155 = f32[2,16,32,4,8,16]{2,5,4,3,1,0:T(8,128)} copy(f32[2,16,32,4,8,16]{2,5,3,4,1,0:T(8,128)} %bitcast.320) | data formatting | bytes 4194304 | tf_op jit(solution)/shard_map/while/body/eval_jaxpr/transpose | solution.py:78
  290.5 5.6 copy.156
  301.3 2.0 copy-done.3
  303.5 2.4 fusion.346
  305.9 2.5 fusion.344
  308.4 2.5 fusion.347
  310.9 2.5 fusion.345
  313.5 7.5 %copy.142 = f32[2,16,32,4,128]{2,1,0,4,3:T(8,128)} copy(f32[2,16,32,4,128]{4,2,1,3,0:T(8,128)S(1)} %maximum_bitcast_fusion.2) | data formatting | bytes 4194304 | tf_op jit(solution)/shard_map/while/body/eval_jaxpr/reshape | solution.py:52
  321.0 6.1 reshape.143
  327.2 29.1 %all_to_all.204 = f32[4,1,131072]{2,1,0:T(1,128)} all-to-all(f32[4,1,131072]{2,1,0:T(1,128)S(1)} %reshape.143), channel_id=1, replica_groups=mesh['py'=4,'pz'=8] {'py'}, dimensions={0} | all-to-all | bytes 4194304 | tf_op jit(solution)/shard_map/while/body/eval_jaxpr/all_to_all | solution.py:54
  356.8 7.7 %reduce.4 = f32[4,131072]{1,0:T(4,128)S(1)} reduce(f32[4,1,131072]{2,1,0:T(1,128)} %all_to_all.204, f32[]{:T(128)} %broadcast.656), dimensions={1}, to_apply=%all_to_all.178.reduce_sub_computation | reduce | bytes 4194308 | tf_op jit(solution)/shard_map/while/body/eval_jaxpr/all_to_all | solution.py:54
  364.5 6.1 reshape.144
  370.6 5.2 copy.143
  377.5 3.1 copy.145
  380.5 4.0 all-to-all-start.1
  385.6 46.7 %all-to-all-done.1 = f32[2,16,128,128]{2,1,0,3:T(8,128)S(1)} async-done(((f32[2,16,128,128]{2,1,0,3:T(8,128)}), f32[2,16,128,128]{2,1,0,3:T(8,128)S(1)}, u32[]{:S(2)}, u32[]{:S(2)}) %all-to-all-start.1) | async-done | bytes 2097184 | tf_op jit(solution)/shard_map/while/body/eval_jaxpr/all_to_all | solution.py:53
  436.4 2.2 fusion.349
  441.3 2.4 fusion.350
  448.9 2.1 fusion.354
  462.2 2.0 fusion.365
  464.2 1.9 fusion.367
  467.6 28.1 %all_to_all.205 = f32[2,128,128,16]{1,3,0,2:T(8,128)S(1)} all-to-all(f32[2,128,128,16]{1,3,0,2:T(8,128)S(1)} %copy.151), channel_id=1, replica_groups=mesh['py'=4,'pz'=8] {'py'}, dimensions={2} | all-to-all | bytes 4194304 | tf_op jit(solution)/shard_map/while/body/eval_jaxpr/all_to_all | solution.py:71
  496.0 4.5 copy.153
  500.5 7.2 %reshape.145 = f32[8,1,65536]{2,1,0:T(1,128)} reshape(f32[128,2,32,64]{3,2,1,0:T(8,128)} %bitcast.327) | data formatting | bytes 4194304 | tf_op jit(solution)/shard_map/while
  507.7 3.9 all-to-all-start.3
  511.6 48.0 %all-to-all-done.3 = f32[8,1,65536]{2,1,0:T(1,128)S(1)} async-done(((f32[8,1,65536]{2,1,0:T(1,128)}), f32[8,1,65536]{2,1,0:T(1,128)S(1)}, u32[]{:S(2)}, u32[]{:S(2)}) %all-to-all-start.3) | async-done | bytes 2097184 | tf_op jit(solution)/shard_map/while/body/eval_jaxpr/all_to_all | solution.py:70
  561.5 7.2 %reduce.5 = f32[8,65536]{1,0:T(8,128)S(1)} reduce(f32[8,1,65536]{2,1,0:T(1,128)} %copy-done, f32[]{:T(128)} %broadcast.657), dimensions={1}, to_apply=%all_to_all.189.reduce_sub_computation | reduce | bytes 4194308 | tf_op jit(solution)/shard_map/while/body/eval_jaxpr/all_to_all | solution.py:70
  568.7 3.6 reshape.146
  572.3 7.0 %copy.154 = f32[2,16,32,8,64]{2,4,3,1,0:T(8,128)} copy(f32[2,16,32,8,64]{4,2,0,1,3:T(8,128)} %bitcast.326) | data formatting | bytes 4194304 | tf_op jit(solution)/shard_map/while/body/eval_jaxpr/all_to_all | solution.py:70
  579.3 7.9 %copy.155 = f32[2,16,32,4,8,16]{2,5,4,3,1,0:T(8,128)} copy(f32[2,16,32,4,8,16]{2,5,3,4,1,0:T(8,128)} %bitcast.320) | data formatting | bytes 4194304 | tf_op jit(solution)/shard_map/while/body/eval_jaxpr/transpose | solution.py:78
  587.2 5.6 copy.156
  598.0 2.0 copy-done.3
  603.1 6.5 multiply_reduce_fusion.1
  609.6 37.5 %all-reduce = (f32[8]{0:T(128)S(1)}, f32[8]{0:T(128)S(1)}) all-reduce(f32[8]{0:T(128)S(1)} %get-tuple-element.349, f32[8]{0:T(128)S(1)} %get-tuple-element.348), channel_id=1, replica_groups=mesh['py'=4,'pz'=8] {'py','pz'}, use_global_device_ids=true, to_apply=%region_3.4 | all-reduce | flops 16 | bytes 128 | tf_op jit(solution)/shard_map/psum | solution.py:101
  647.2 4.2 multiply_reduce_fusion
  651.4 41.5 %psum.23 = f32[8]{0:T(128)S(1)} all-reduce(f32[8]{0:T(128)S(1)} %multiply_reduce_fusion), channel_id=1, replica_groups=mesh['py'=4,'pz'=8] {'py','pz'}, use_global_device_ids=true, to_apply=%region_7.8 | all-reduce | flops 8 | bytes 64 | tf_op jit(solution)/shard_map/psum | solution.py:104
  (90 shorter events, 70.7 us)
Async XLA Ops:
  3.2 599.9 %copy-start.4 = (f32[16,32,128]{2,1,0:T(8,128)S(1)}, f32[16,32,128]{2,1,0:T(8,128)}, u32[]{:S(2)}) copy-start(f32[16,32,128]{2,1,0:T(8,128)} %param.7) | copy-start | bytes 786436
  81.3 54.2 %all-to-all-start.1 = ((f32[2,16,128,128]{2,1,0,3:T(8,128)}), f32[2,16,128,128]{2,1,0,3:T(8,128)S(1)}, u32[]{:S(2)}, u32[]{:S(2)}) async-start(f32[2,16,128,128]{2,1,0,3:T(8,128)} %copy.145), calls=%async_computation.1 | async-start | bytes 4194304 | tf_op jit(solution)/shard_map/while/body/eval_jaxpr/all_to_all | solution.py:53
  138.5 3.5 copy-start.1
  211.0 51.9 %all-to-all-start.3 = ((f32[8,1,65536]{2,1,0:T(1,128)}), f32[8,1,65536]{2,1,0:T(1,128)S(1)}, u32[]{:S(2)}, u32[]{:S(2)}) async-start(f32[8,1,65536]{2,1,0:T(1,128)} %reshape.145), calls=%async_computation.3 | async-start | bytes 4194304 | tf_op jit(solution)/shard_map/while/body/eval_jaxpr/all_to_all | solution.py:70
  262.9 1.4 copy-start
  298.6 2.5 copy-start.2
  301.3 2.0 copy-start.3
  380.5 51.7 %all-to-all-start.1 = ((f32[2,16,128,128]{2,1,0,3:T(8,128)}), f32[2,16,128,128]{2,1,0,3:T(8,128)S(1)}, u32[]{:S(2)}, u32[]{:S(2)}) async-start(f32[2,16,128,128]{2,1,0,3:T(8,128)} %copy.145), calls=%async_computation.1 | async-start | bytes 4194304 | tf_op jit(solution)/shard_map/while/body/eval_jaxpr/all_to_all | solution.py:53
  435.2 3.5 copy-start.1
  507.7 51.9 %all-to-all-start.3 = ((f32[8,1,65536]{2,1,0:T(1,128)}), f32[8,1,65536]{2,1,0:T(1,128)S(1)}, u32[]{:S(2)}, u32[]{:S(2)}) async-start(f32[8,1,65536]{2,1,0:T(1,128)} %reshape.145), calls=%async_computation.3 | async-start | bytes 4194304 | tf_op jit(solution)/shard_map/while/body/eval_jaxpr/all_to_all | solution.py:70
  559.6 1.4 copy-start
  595.2 2.5 copy-start.2
  598.0 2.0 copy-start.3
  647.1 4.2 copy-start.5
  647.2 45.7 %copy-start.6 = (s32[8]{0:T(128)S(1)}, s32[8]{0:T(128)}, u32[]{:S(2)}) copy-start(s32[8]{0:T(128)} %param.9) | copy-start | bytes 100
where the time goes:
time: 697 us; the launch traced here: 694 us
  blocking collectives  195 us (28%)
  waiting for transfers between devices  189 us (27%)
  local copies, waits for them, and re-layouts  156 us (22%)
  matrix products  85.4 us (12%)
  other arithmetic  44.8 us (6%)
  starting transfers between devices  18.7 us (3%)
    all_to_all x2, waiting for transfers between devices, slab_kinetic(): lax.all_to_all(lax.all_to_all(spatial, 'py', split_axis=2, concat_axis=3,...  96 us
    all_to_all x2, waiting for transfers between devices, slab_kinetic(): lax.all_to_all(lax.all_to_all(flat, 'py', split_axis=3, concat_axis=2, ti...  92.9 us
    all_to_all x2, blocking collectives, slab_kinetic(): lax.all_to_all(flat, 'py', split_axis=3, concat_axis=2, tiled=True)  59.3 us
    all_to_all x2, blocking collectives, slab_kinetic(): lax.all_to_all(spatial, 'py', split_axis=2, concat_axis=3, tiled=True)  56.3 us
    while x24, local copies, waits for them, and re-layouts  52.9 us
    psum x1, blocking collectives, body(): lax.psum(jnp.sum(residual * residual, axis=(0, 2, 3, 4)), ('py', 'pz'))  41.5 us
    psum x1, blocking collectives, body(): lax.psum((norm_local, correlation_local), ('py', 'pz'))  37.5 us
    dot_general x12, matrix products, transform_axis(): jnp.einsum(form, imag_part, sines, precision=high)  22.5 us
  transfers between devices with their start and end apart: 4, of which 4 were waited for; matrix products, arithmetic and copies ran while one was open for 0% of the time, Pallas kernels for 0%

commit v1 on v0

--- a/solution.py
+++ b/solution.py
@@ -3,6 +3,17 @@
 import jax.numpy as jnp
 from jax import lax
 from jax.sharding import PartitionSpec as P
+from jax.lax import all_to_all, axis_size
+
+render_the_spot = lambda local: jnp.concatenate(
+    all_to_all(
+        jnp.stack(jnp.split(local, axis_size("py"), axis=3), axis=0),
+        axis_name="py",
+        split_axis=0,
+        concat_axis=0,
+    ),
+    axis=2,
+)
 
 
 def make_tables(length, inverse):
@@ -50,13 +61,7 @@
     size_z = lax.axis_size("pz")
     along_x = transform_axis(field, 4, forward)
     flat = jnp.moveaxis(along_x, 1, 3).reshape(parts, rows_z, rows_y, bands * length)
-    planes = lax.all_to_all(
-        lax.all_to_all(flat, "py", split_axis=3, concat_axis=2, tiled=True),
-        "pz",
-        split_axis=3,
-        concat_axis=1,
-        tiled=True,
-    )
+    planes = lax.all_to_all(render_the_spot(flat), "pz", split_axis=3, concat_axis=1, tiled=True)
     width = planes.shape[3]
     start = lax.axis_index("py") * (bands * length // size_y) + lax.axis_index("pz") * width
     column = start + jnp.arange(width, dtype=jnp.int32)

time: 697 us -> 625 us (0.90)
  local copies, waits for them, and re-layouts: 156 us -> 101 us
  other arithmetic: 44.8 us -> 29.9 us
    while x24 -> x20, local copies, waits for them, and re-layouts: 52.9 us -> 28.4 us
    all_to_all x10 -> x2, local copies, waits for them, and re-layouts: 23.3 us -> 2.43 us  [slab_kinetic(): lax.all_to_all(render_the_spot(flat), 'pz', split_axis=3, concat_axis=1,...]
    all_to_all x2 -> x0, other arithmetic: 15.4 us -> none  [slab_kinetic(): lax.all_to_all(flat, 'py', split_axis=3, concat_axis=2, tiled=True)]
    reshape x2 -> x4, local copies, waits for them, and re-layouts: 15 us -> 4.54 us  [jnp.concatenate(all_to_all(jnp.stack(jnp.split(local, axis_size('py'), ax...]
where the time goes in v1:
time: 625 us; the launch traced here: 622 us
  blocking collectives  193 us (31%)
  waiting for transfers between devices  189 us (30%)
  local copies, waits for them, and re-layouts  101 us (16%)
  matrix products  85.5 us (14%)
  other arithmetic  29.9 us (5%)
  starting transfers between devices  17.8 us (3%)
    all_to_all x2, waiting for transfers between devices, slab_kinetic(): lax.all_to_all(lax.all_to_all(spatial, 'py', split_axis=2, concat_axis=3,...  96 us
    all_to_all x2, waiting for transfers between devices, slab_kinetic(): lax.all_to_all(render_the_spot(flat), 'pz', split_axis=3, concat_axis=1,...  93.3 us
    all_to_all x2, blocking collectives, all_to_all(jnp.stack(jnp.split(local, axis_size('py'), axis=3), axis=0),...  57.9 us
    all_to_all x2, blocking collectives, slab_kinetic(): lax.all_to_all(spatial, 'py', split_axis=2, concat_axis=3, tiled=True)  56.3 us
    psum x1, blocking collectives, body(): lax.psum(jnp.sum(residual * residual, axis=(0, 2, 3, 4)), ('py', 'pz'))  41.5 us
    psum x1, blocking collectives, body(): lax.psum((norm_local, correlation_local), ('py', 'pz'))  37.5 us
    while x20, local copies, waits for them, and re-layouts  28.4 us
    dot_general x12, matrix products, transform_axis(): jnp.einsum(form, imag_part, sines, precision=high)  22.5 us
  transfers between devices with their start and end apart: 4, of which 4 were waited for; matrix products, arithmetic and copies ran while one was open for 0% of the time, Pallas kernels for 0%

profile of v1, /device:TPU:0, one launch (start us, length us, event | category | flops | bytes accessed | tf_op | source)
XLA Modules:
  0.0 621.8 jit_solution(10258507837565134379)
XLA Ops:
  0.6 2.5 broadcast_in_dim.14
  3.2 527.9 %while.18 = (s32[]{:T(128)}, f32[2,8,16,32,128]{4,3,2,1,0:T(8,128)}, f32[2,8,16,32,128]{4,3,2,1,0:T(8,128)}, s32[1]{0:T(128)}, s32[]{:T(128)}, /*index=5*/s32[]{...) while((s32[]{:T(128)}, ...), condition=%wide.region_1.2_spmd.clone.clone, body=%wide.region_0.1_spmd.clone.clone.sunk | while | flops 9678143488 | bytes 220333664 | solution.py:102
  3.2 2.5 fusion.346
  5.7 2.4 fusion.344
  8.1 2.5 fusion.347
  10.6 2.5 fusion.345
  13.8 29.7 %all_to_all.164 = f32[4,2,16,32,128]{4,3,2,1,0:T(8,128)S(1)} all-to-all(f32[4,2,16,32,128]{4,3,2,1,0:T(8,128)S(1)} %pad_maximum_fusion.4), channel_id=1, replica_groups=mesh['py'=4,'pz'=8] {'py'}, dimensions={0} | all-to-all | bytes 4194304 | tf_op jit(solution)/shard_map/while/body/eval_jaxpr/all_to_all | solution.py:9
  43.8 2.1 copy.140
  45.9 6.2 %all-to-all-start.1 = ((f32[2,16,128,128]{2,1,0,3:T(8,128)}), f32[2,16,128,128]{2,1,0,3:T(8,128)S(1)}, u32[]{:S(2)}, u32[]{:S(2)}) async-start(f32[2,16,128,128]{2,1,0,3:T(8,128)} %copy.140), calls=%async_computation.1 | async-start | bytes 4194304 | tf_op jit(solution)/shard_map/while/body/eval_jaxpr/all_to_all | solution.py:64
  53.1 46.4 %all-to-all-done.1 = f32[2,16,128,128]{2,1,0,3:T(8,128)S(1)} async-done(((f32[2,16,128,128]{2,1,0,3:T(8,128)}), f32[2,16,128,128]{2,1,0,3:T(8,128)S(1)}, u32[]{:S(2)}, u32[]{:S(2)}) %all-to-all-start.1) | async-done | bytes 2097184 | tf_op jit(solution)/shard_map/while/body/eval_jaxpr/all_to_all | solution.py:64
  103.7 2.2 fusion.349
  108.6 2.4 fusion.350
  111.1 1.9 fusion.355
  113.0 1.9 fusion.351
  116.2 2.1 fusion.354
  118.3 1.9 fusion.356
  124.2 1.9 fusion.366
  126.1 1.9 fusion.362
  129.5 2.0 fusion.365
  131.5 1.9 fusion.367
  134.9 28.1 %all_to_all.165 = f32[2,128,128,16]{1,3,0,2:T(8,128)S(1)} all-to-all(f32[2,128,128,16]{1,3,0,2:T(8,128)S(1)} %copy.146), channel_id=1, replica_groups=mesh['py'=4,'pz'=8] {'py'}, dimensions={2} | all-to-all | bytes 4194304 | tf_op jit(solution)/shard_map/while/body/eval_jaxpr/all_to_all | solution.py:76
  163.3 4.5 copy.148
  167.8 7.2 %reshape.165 = f32[8,1,65536]{2,1,0:T(1,128)} reshape(f32[128,2,32,64]{3,2,1,0:T(8,128)} %bitcast.329) | data formatting | bytes 4194304 | tf_op jit(solution)/shard_map/while
  175.0 3.9 all-to-all-start.3
  178.9 48.0 %all-to-all-done.3 = f32[8,1,65536]{2,1,0:T(1,128)S(1)} async-done(((f32[8,1,65536]{2,1,0:T(1,128)}), f32[8,1,65536]{2,1,0:T(1,128)S(1)}, u32[]{:S(2)}, u32[]{:S(2)}) %all-to-all-start.3) | async-done | bytes 2097184 | tf_op jit(solution)/shard_map/while/body/eval_jaxpr/all_to_all | solution.py:75
  228.8 7.2 %reduce.2 = f32[8,65536]{1,0:T(8,128)S(1)} reduce(f32[8,1,65536]{2,1,0:T(1,128)} %copy-done, f32[]{:T(128)} %broadcast.654), dimensions={1}, to_apply=%all_to_all.149.reduce_sub_computation | reduce | bytes 4194308 | tf_op jit(solution)/shard_map/while/body/eval_jaxpr/all_to_all | solution.py:75
  236.0 3.6 reshape.166
  239.6 7.0 %copy.149 = f32[2,16,32,8,64]{2,4,3,1,0:T(8,128)} copy(f32[2,16,32,8,64]{4,2,0,1,3:T(8,128)} %bitcast.328) | data formatting | bytes 4194304 | tf_op jit(solution)/shard_map/while/body/eval_jaxpr/all_to_all | solution.py:75
  246.6 7.9 %copy.150 = f32[2,16,32,4,8,16]{2,5,4,3,1,0:T(8,128)} copy(f32[2,16,32,4,8,16]{2,5,3,4,1,0:T(8,128)} %bitcast.322) | data formatting | bytes 4194304 | tf_op jit(solution)/shard_map/while/body/eval_jaxpr/transpose | solution.py:83
  254.5 5.6 copy.151
  265.3 2.0 copy-done.3
  267.5 2.4 fusion.346
  269.9 2.5 fusion.344
  272.4 2.5 fusion.347
  274.9 2.5 fusion.345
  278.1 28.1 %all_to_all.164 = f32[4,2,16,32,128]{4,3,2,1,0:T(8,128)S(1)} all-to-all(f32[4,2,16,32,128]{4,3,2,1,0:T(8,128)S(1)} %pad_maximum_fusion.4), channel_id=1, replica_groups=mesh['py'=4,'pz'=8] {'py'}, dimensions={0} | all-to-all | bytes 4194304 | tf_op jit(solution)/shard_map/while/body/eval_jaxpr/all_to_all | solution.py:9
  306.5 2.1 copy.140
  308.5 3.8 all-to-all-start.1
  313.3 46.8 %all-to-all-done.1 = f32[2,16,128,128]{2,1,0,3:T(8,128)S(1)} async-done(((f32[2,16,128,128]{2,1,0,3:T(8,128)}), f32[2,16,128,128]{2,1,0,3:T(8,128)S(1)}, u32[]{:S(2)}, u32[]{:S(2)}) %all-to-all-start.1) | async-done | bytes 2097184 | tf_op jit(solution)/shard_map/while/body/eval_jaxpr/all_to_all | solution.py:64
  364.4 2.2 fusion.349
  369.3 2.4 fusion.350
  371.8 1.9 fusion.355
  373.7 1.9 fusion.351
  376.8 2.4 fusion.354
  379.2 1.9 fusion.356
  385.1 1.9 fusion.366
  387.0 1.9 fusion.362
  390.4 2.0 fusion.365
  392.3 1.9 fusion.367
  395.7 28.1 %all_to_all.165 = f32[2,128,128,16]{1,3,0,2:T(8,128)S(1)} all-to-all(f32[2,128,128,16]{1,3,0,2:T(8,128)S(1)} %copy.146), channel_id=1, replica_groups=mesh['py'=4,'pz'=8] {'py'}, dimensions={2} | all-to-all | bytes 4194304 | tf_op jit(solution)/shard_map/while/body/eval_jaxpr/all_to_all | solution.py:76
  424.1 4.5 copy.148
  428.6 7.2 %reshape.165 = f32[8,1,65536]{2,1,0:T(1,128)} reshape(f32[128,2,32,64]{3,2,1,0:T(8,128)} %bitcast.329) | data formatting | bytes 4194304 | tf_op jit(solution)/shard_map/while
  435.8 3.9 all-to-all-start.3
  439.7 48.0 %all-to-all-done.3 = f32[8,1,65536]{2,1,0:T(1,128)S(1)} async-done(((f32[8,1,65536]{2,1,0:T(1,128)}), f32[8,1,65536]{2,1,0:T(1,128)S(1)}, u32[]{:S(2)}, u32[]{:S(2)}) %all-to-all-start.3) | async-done | bytes 2097184 | tf_op jit(solution)/shard_map/while/body/eval_jaxpr/all_to_all | solution.py:75
  489.6 7.2 %reduce.2 = f32[8,65536]{1,0:T(8,128)S(1)} reduce(f32[8,1,65536]{2,1,0:T(1,128)} %copy-done, f32[]{:T(128)} %broadcast.654), dimensions={1}, to_apply=%all_to_all.149.reduce_sub_computation | reduce | bytes 4194308 | tf_op jit(solution)/shard_map/while/body/eval_jaxpr/all_to_all | solution.py:75
  496.8 3.6 reshape.166
  500.4 7.0 %copy.149 = f32[2,16,32,8,64]{2,4,3,1,0:T(8,128)} copy(f32[2,16,32,8,64]{4,2,0,1,3:T(8,128)} %bitcast.328) | data formatting | bytes 4194304 | tf_op jit(solution)/shard_map/while/body/eval_jaxpr/all_to_all | solution.py:75
  507.4 7.9 %copy.150 = f32[2,16,32,4,8,16]{2,5,4,3,1,0:T(8,128)} copy(f32[2,16,32,4,8,16]{2,5,3,4,1,0:T(8,128)} %bitcast.322) | data formatting | bytes 4194304 | tf_op jit(solution)/shard_map/while/body/eval_jaxpr/transpose | solution.py:83
  515.3 5.4 copy.151
  525.9 2.0 copy-done.3
  531.1 6.5 %multiply_reduce_fusion.1 = (f32[8]{0:T(128)S(1)}, f32[8]{0:T(128)S(1)}, f32[2,8,16,32,128]{4,3,2,1,0:T(8,128)}) fusion(f32[2,8,16,32,128]{4,3,2,1,0:T(8,128)} %get-tuple-element.450, f32[2,8,16,32,128]{4,3,2,1,0:T(8,128)} %get-tuple-element.289, f32[16,32,128]{2,1,0:T(8,128)S(1)} %copy-done.4), kind=kLoop, calls=%fused_computation.243 | loop fusion | flops 6291440 | bytes 12845120 | tf_op jit(solution)/shard_map/reduce_sum | solution.py:104
  537.6 37.5 %all-reduce = (f32[8]{0:T(128)S(1)}, f32[8]{0:T(128)S(1)}) all-reduce(f32[8]{0:T(128)S(1)} %get-tuple-element.349, f32[8]{0:T(128)S(1)} %get-tuple-element.348), channel_id=1, replica_groups=mesh['py'=4,'pz'=8] {'py','pz'}, use_global_device_ids=true, to_apply=%region_3.4 | all-reduce | flops 16 | bytes 128 | tf_op jit(solution)/shard_map/psum | solution.py:106
  575.2 4.2 multiply_reduce_fusion
  579.4 41.5 %psum.23 = f32[8]{0:T(128)S(1)} all-reduce(f32[8]{0:T(128)S(1)} %multiply_reduce_fusion), channel_id=1, replica_groups=mesh['py'=4,'pz'=8] {'py','pz'}, use_global_device_ids=true, to_apply=%region_7.8 | all-reduce | flops 8 | bytes 64 | tf_op jit(solution)/shard_map/psum | solution.py:109
  (82 shorter events, 48.6 us)
Async XLA Ops:
  3.2 527.9 %copy-start.4 = (f32[16,32,128]{2,1,0:T(8,128)S(1)}, f32[16,32,128]{2,1,0:T(8,128)}, u32[]{:S(2)}) copy-start(f32[16,32,128]{2,1,0:T(8,128)} %param.7) | copy-start | bytes 786436
  45.9 53.7 %all-to-all-start.1 = ((f32[2,16,128,128]{2,1,0,3:T(8,128)}), f32[2,16,128,128]{2,1,0,3:T(8,128)S(1)}, u32[]{:S(2)}, u32[]{:S(2)}) async-start(f32[2,16,128,128]{2,1,0,3:T(8,128)} %copy.140), calls=%async_computation.1 | async-start | bytes 4194304 | tf_op jit(solution)/shard_map/while/body/eval_jaxpr/all_to_all | solution.py:64
  102.5 3.5 copy-start.1
  175.0 51.9 %all-to-all-start.3 = ((f32[8,1,65536]{2,1,0:T(1,128)}), f32[8,1,65536]{2,1,0:T(1,128)S(1)}, u32[]{:S(2)}, u32[]{:S(2)}) async-start(f32[8,1,65536]{2,1,0:T(1,128)} %reshape.165), calls=%async_computation.3 | async-start | bytes 4194304 | tf_op jit(solution)/shard_map/while/body/eval_jaxpr/all_to_all | solution.py:75
  226.9 1.4 copy-start
  262.5 2.5 copy-start.2
  265.3 2.0 copy-start.3
  308.5 51.7 %all-to-all-start.1 = ((f32[2,16,128,128]{2,1,0,3:T(8,128)}), f32[2,16,128,128]{2,1,0,3:T(8,128)S(1)}, u32[]{:S(2)}, u32[]{:S(2)}) async-start(f32[2,16,128,128]{2,1,0,3:T(8,128)} %copy.140), calls=%async_computation.1 | async-start | bytes 4194304 | tf_op jit(solution)/shard_map/while/body/eval_jaxpr/all_to_all | solution.py:64
  363.1 3.5 copy-start.1
  435.8 51.9 %all-to-all-start.3 = ((f32[8,1,65536]{2,1,0:T(1,128)}), f32[8,1,65536]{2,1,0:T(1,128)S(1)}, u32[]{:S(2)}, u32[]{:S(2)}) async-start(f32[8,1,65536]{2,1,0:T(1,128)} %reshape.165), calls=%async_computation.3 | async-start | bytes 4194304 | tf_op jit(solution)/shard_map/while/body/eval_jaxpr/all_to_all | solution.py:75
  487.7 1.4 copy-start
  523.1 2.5 copy-start.2
  525.9 2.0 copy-start.3
  575.2 4.2 copy-start.5
  575.2 45.7 %copy-start.6 = (s32[8]{0:T(128)S(1)}, s32[8]{0:T(128)}, u32[]{:S(2)}) copy-start(s32[8]{0:T(128)} %param.9) | copy-start | bytes 100
